TPU v7x, 32 devices: a whole 2x2x4 slice. The times are simulated.
32 devices in a mesh: blk: 8 (over z, y), plane: 4 (over x, core).
Axes of the slice: x: 2, y: 2, z: 4, core: 2. Of those that a mesh axis runs over, the one named last changes fastest.
Arguments:
- tiles: bfloat16 [128, 24, 128, 128], P(('blk', 'plane')), may hold values from -0.25 to 0.25
- tile_cols: int32 [128, 24], P(('blk', 'plane')), may hold values from 0 to 511
- tile_count: int32 [128], P(('blk', 'plane')), may hold values from 18 to 24, as said below
- u_start: float32 [16384], P(('blk', 'plane')), may hold values from -0.046875 to 0.046875
- v_start: float32 [65536], P(('blk', 'plane')), may hold values from -0.0234375 to 0.0234375
- beta_start: float32 [1], replicated, may hold values from 0.5 to 1.5
- left_basis: float32 [16384, 128], P(('blk', 'plane')), may hold values from -0.046875 to 0.046875
- right_basis: float32 [65536, 128], P(('blk', 'plane')), may hold values from -0.0234375 to 0.0234375
Outputs:
- left_vectors: float32 [1, 16384], P(None, ('blk', 'plane'))
- right_vectors: float32 [1, 65536], P(None, ('blk', 'plane'))
- coefficients: float32 [2], replicated
Inputs may be any that keep to these rules, and one draw needn't show every extreme that they name: `tile_count`: slots at and after a row block's count are padding; some row block uses all 24 slots.
All inputs are finite; a program needn't handle non-finite values.
Results may differ from a plain program's by a relative error of at most 0.00055.
The roundings to bfloat16 on the way count: a program that leaves them out, or rounds other values in their place, can miss the bound.
Values may be sent and summed in bfloat16 or wider, within the bound.
A program may use at most 64 MiB of HBM per device.

v0:
```python
import math

import jax
import jax.numpy as jnp
from jax import lax
from jax.sharding import PartitionSpec as P


def project_twice(vec, basis, gram):
    high = lax.Precision.HIGHEST
    first, whole_sq = lax.psum(
        (jnp.dot(vec, basis, precision=high), jnp.sum(vec * vec)), ("blk", "plane")
    )
    coef = 2.0 * first - jnp.dot(gram, first, precision=high)
    vec = vec - jnp.dot(basis, coef, precision=high)
    total = (
        whole_sq - 2.0 * jnp.sum(coef * first) + jnp.sum(coef * jnp.dot(gram, coef, precision=high))
    )
    norm = jnp.sqrt(total + 1e-06)
    return (vec / norm, norm)


def on_device(tiles, tile_cols, tile_count, u_start, v_start, beta_start, left_basis, right_basis):
    high = lax.Precision.HIGHEST
    devices = lax.axis_size(("blk", "plane"))
    blocks, slots = tile_cols.shape
    n_tiles = v_start.shape[0] * devices // 128
    live = (lax.iota(jnp.int32, slots)[None, :] < tile_count[:, None]).astype(jnp.float32)
    onehot = (tile_cols.reshape(-1)[:, None] == lax.iota(jnp.int32, n_tiles)[None, :]).astype(
        jnp.float32
    )
    left_gram, right_gram = lax.psum(
        (
            jnp.dot(left_basis.T, left_basis, precision=high),
            jnp.dot(right_basis.T, right_basis, precision=high),
        ),
        ("blk", "plane"),
    )
    left_scale = math.sqrt(u_start.shape[0] * devices)
    right_scale = math.sqrt(v_start.shape[0] * devices)
    vec_right = v_start
    vec_left = u_start
    beta = beta_start[0]
    lefts, rights, coefs = ([], [], [])
    rounded = vec_right.astype(jnp.bfloat16)
    whole = lax.all_gather(rounded, ("blk", "plane"), axis=0, tiled=True)
    table = whole.reshape(n_tiles, 128)
    picked = jnp.take(table, tile_cols, axis=0)
    values = jnp.einsum("rsij,rsj->rsi", tiles, picked, preferred_element_type=jnp.float32)
    forward_out = jnp.sum(values * live[:, :, None], axis=1).reshape(-1)
    vec_left, alpha = project_twice(forward_out - beta * vec_left, left_basis, left_gram)
    left_rows = vec_left.astype(jnp.bfloat16).reshape(blocks, 128)
    contrib = jnp.einsum("rsij,ri->rsj", tiles, left_rows, preferred_element_type=jnp.float32)
    contrib = (contrib * live[:, :, None]).reshape(-1, 128)
    partial_value = lax.dot_general(onehot, contrib, (((0,), (0,)), ((), ())), precision=high)
    owned = lax.psum_scatter(partial_value, ("blk", "plane"), scatter_dimension=0, tiled=True)
    back_out = owned.reshape(-1)
    vec_right, beta = project_twice(back_out - alpha * vec_right, right_basis, right_gram)
    lefts.append(vec_left * left_scale)
    rights.append(vec_right * right_scale)
    coefs.append(alpha)
    coefs.append(beta)
    return (jnp.stack(lefts), jnp.stack(rights), jnp.stack(coefs))


def solution(mesh):
    placed = (
        P(("blk", "plane"), None, None, None),
        P(("blk", "plane"), None),
        P(("blk", "plane")),
        P(("blk", "plane")),
        P(("blk", "plane")),
        P(),
        P(("blk", "plane"), None),
        P(("blk", "plane"), None),
    )
    return jax.shard_map(
        on_device,
        mesh=mesh,
        in_specs=placed,
        out_specs=(P(None, ("blk", "plane")), P(None, ("blk", "plane")), P()),
        check_vma=False,
    )
```

profile of v0, /device:TPU:0, one launch (start us, length us, event | category | flops | bytes accessed | tf_op | source)
XLA Modules:
  0.0 338.0 jit_solution(10103056694969738724)
XLA Ops:
  7.2 2.4 fusion.21
  9.6 4.1 %fusion.22 = f32[128,128]{1,0:T(8,128)} fusion(f32[2048,128]{1,0:T(8,128)} %param.15), kind=kOutput, calls=%fused_computation.48 | convolution fusion | flops 402653184 | bytes 1114112 | tf_op jit(solution)/shard_map/dot_general | solution.py:35
  13.8 0.7 compare_and_fusion
  14.5 0.8 eq.15
  15.2 0.7 compare_select_fusion
  16.6 0.7 fusion.12
  17.3 0.1 reshape.56
  17.4 0.7 convert_element_type.14
  18.1 43.6 %all_gather.3 = bf16[65536]{0:T(1024)(128)(2,1)S(1)} all-gather(bf16[2048]{0:T(1024)(128)(2,1)S(1)} %convert_element_type.14), channel_id=1, replica_groups=mesh['blk'=8,'plane'=4] {'blk','plane'}, dimensions={0}, use_global_device_ids=true | all-gather | bytes 135168 | tf_op jit(solution)/shard_map/all_gather | solution.py:46
  61.7 1.3 gather_fusion
  62.9 0.8 select_bitcast_fusion
  63.8 1.7 fusion.8
  65.5 0.1 multiply_reduce_fusion
  65.6 1.3 multiply_reduce_fusion.2
  66.9 0.2 convolution_bitcast_fusion.1
  67.1 37.2 %all-reduce.1 = (f32[128]{0:T(128)S(1)}, f32[]{:T(128)}) all-reduce(f32[128]{0:T(128)S(1)} %convolution_bitcast_fusion.1, f32[]{:T(128)} %get-tuple-element.13), channel_id=1, replica_groups=mesh['blk'=8,'plane'=4] {'blk','plane'}, use_global_device_ids=true, to_apply=%region_1.0 | all-reduce | flops 129 | bytes 1032 | tf_op jit(solution)/shard_map/psum | solution.py:11
  104.3 37.2 %all-reduce.5.cloned.1.call-done = (f32[128,128]{1,0:T(8,128)}, f32[128,128]{1,0:T(8,128)}) async-done(((f32[128,128]{1,0:T(8,128)}, f32[128,128]{1,0:T(8,128)}), (f32[128,128]{1,0:T(8,128)}, f32[128,128]{1,0:T(8,128)})) %all-reduce.5.cloned.1.call-update) | async-done | bytes 131088 | tf_op jit(solution)/shard_map/psum | solution.py:32
  141.5 1.7 multiply_reduce_fusion.4
  143.2 1.7 fusion.4
  144.9 0.3 fusion.18
  147.2 0.5 fusion.10
  147.8 1.2 fusion.6
  149.0 0.6 broadcast_multiply_fusion.1
  149.6 134.2 %reduce-scatter.2.cloned.1.call-done = f32[16,128]{1,0:T(8,128)} async-done(((f32[512,128]{1,0:T(8,128)}), f32[16,128]{1,0:T(8,128)}) %reduce-scatter.2.cloned.1.call-update) | async-done | bytes 8208 | tf_op jit(solution)/shard_map/reduce_scatter | solution.py:56
  283.8 1.3 multiply_reduce_fusion.1
  285.1 1.8 convolution_bitcast_fusion
  286.9 37.1 %all-reduce = (f32[128]{0:T(128)S(1)}, f32[]{:T(128)}) all-reduce(f32[128]{0:T(128)S(1)} %convolution_bitcast_fusion, f32[]{:T(128)} %get-tuple-element.9), channel_id=1, replica_groups=mesh['blk'=8,'plane'=4] {'blk','plane'}, use_global_device_ids=true, to_apply=%region_8.9 | all-reduce | flops 129 | bytes 1032 | tf_op jit(solution)/shard_map/psum | solution.py:11
  324.0 0.8 multiply_reduce_fusion.3
  324.9 0.9 fusion.5
  325.8 2.2 fusion.14
  330.0 0.6 divide_multiply_fusion
  330.6 0.6 pad_maximum_fusion
  (15 shorter events, 0.2 us)
Async XLA Ops:
  7.2 56.6 %copy-start = (bf16[4,24,128,128]{3,2,1,0:T(8,128)(2,1)S(1)}, bf16[4,24,128,128]{3,2,1,0:T(8,128)(2,1)}, u32[]{:S(2)}) copy-start(bf16[4,24,128,128]{3,2,1,0:T(8,128)(2,1)} %param.8) | copy-start | bytes 9437188
  7.2 134.3 %all-reduce.5.cloned.1.call-start = ((), (), s32[]{:S(2)}) async-start(), calls=%async_computation.2 | async-start | bytes 262144 | tf_op jit(solution)/shard_map/psum | solution.py:32
  9.6 57.3 %copy-start.1 = (f32[512,128]{1,0:T(8,128)S(1)}, f32[512,128]{1,0:T(8,128)}, u32[]{:S(2)}) copy-start(f32[512,128]{1,0:T(8,128)} %param.14) | copy-start | bytes 786436
  13.7 270.1 %reduce-scatter.2.cloned.1.call-start = ((), (), s32[]{:S(2)}) async-start(), calls=%async_computation.1 | async-start | bytes 270336 | tf_op jit(solution)/shard_map/reduce_scatter | solution.py:56
  63.8 220.0 %copy-start.3 = (f32[2048]{0:T(1024)S(1)}, f32[2048]{0:T(1024)}, u32[]{:S(2)}) copy-start(f32[2048]{0:T(1024)} %param.12) | copy-start | bytes 24580
  141.5 182.5 %copy-start.2 = (f32[128,128]{1,0:T(8,128)S(1)}, f32[128,128]{1,0:T(8,128)}, u32[]{:S(2)}) copy-start(f32[128,128]{1,0:T(8,128)} %get-tuple-element.8) | copy-start | bytes 196612
Sparse Core Ops, SparseCore 0:
  13.9 127.5 all-reduce.4
  149.1 134.6 reduce-scatter.1
where the time goes:
time: 340 us; the launch traced here: 338 us
  waiting for transfers between devices  171 us (50%)
  blocking collectives  118 us (35%)
  matrix products  19.5 us (6%)
  between operations  18.8 us (6%)
  other arithmetic  8.19 us (2%)
    reduce_scatter x1, waiting for transfers between devices, on_device(): lax.psum_scatter(partial_value, ('blk', 'plane'), scatter_dimension=0, ti...  134 us
    psum x2, blocking collectives, project_twice(): lax.psum((jnp.dot(vec, basis, precision=high), jnp.sum(vec * vec)), ('blk...  74.3 us
    all_gather x1, blocking collectives, on_device(): whole = lax.all_gather(rounded, ('blk', 'plane'), axis=0, tiled=True)  43.6 us
    psum x1, waiting for transfers between devices, on_device(): lax.psum((jnp.dot(left_basis.T, left_basis, precision=high), jnp.dot(righ...  37.2 us
  transfers between devices with their start and end apart: 2, of which 2 were waited for; matrix products, arithmetic and copies ran while one was open for 3% of the time, Pallas kernels for 0%

commit v1 on v0

v1 whole, which is shorter than its diff:
```python
import functools
import math

import jax
import jax.numpy as jnp
from jax import lax
from jax.experimental import pallas as pl
from jax.experimental.pallas import tpu as pltpu
from jax.sharding import PartitionSpec as P

AXES = ("blk", "plane")
HIGH = lax.Precision.HIGHEST
LANES = 128
NT_DIMS = (((1,), (1,)), ((), ()))


def steps_kernel(
    devices,
    planes,
    own_tiles,
    left_scale,
    right_scale,
    beta_ref,
    count_ref,
    cols_ref,
    u_ref,
    v_ref,
    tiles_hbm,
    left_hbm,
    right_hbm,
    out_left,
    out_right,
    out_coef,
    tiles,
    left,
    right,
    left_t,
    right_t,
    v_send,
    v_all,
    cols_rows,
    pick_hot,
    put_hot,
    picked,
    contrib,
    gram_send,
    gram_recv,
    gram_sum,
    gram_all,
    dot_send,
    dot_recv,
    part_send,
    part_recv,
    own_scr,
    p_scr,
    copy_sem,
    send_sem,
    recv_sem,
):
    blocks, slots = cols_ref.shape
    keep = left.shape[1]
    me_blk, me_plane = lax.axis_index("blk"), lax.axis_index("plane")
    me = me_blk * planes + me_plane
    chunks = gram_send.shape[0]
    pad_tiles = v_send.shape[0]
    part_rows = part_send.shape[1]
    stride = picked.shape[0] // blocks

    def target(step):
        other = lax.rem(me + step, devices)
        return other, (other // planes, lax.rem(other, planes))

    barrier = pltpu.get_barrier_semaphore()

    def greet(step, carry):
        _, place = target(step)
        pl.semaphore_signal(
            barrier, inc=1, device_id=place, device_id_type=pl.DeviceIdType.MESH
        )
        return carry

    lax.fori_loop(1, devices, greet, 0)

    loads = [
        pltpu.make_async_copy(left_hbm, left, copy_sem.at[0]),
        pltpu.make_async_copy(right_hbm, right, copy_sem.at[1]),
        pltpu.make_async_copy(tiles_hbm, tiles, copy_sem.at[2]),
    ]
    for load in loads:
        load.start()

    def send_all(phase, source, landing):
        def body(step, carry):
            other, place = target(step)
            pltpu.make_async_remote_copy(
                src_ref=source(other),
                dst_ref=landing.at[me],
                send_sem=send_sem.at[phase],
                recv_sem=recv_sem.at[phase],
                device_id=place,
                device_id_type=pl.DeviceIdType.MESH,
            ).start()
            return carry

        lax.fori_loop(1, devices, body, 0)

    def wait_all(sem, phase, landing):
        most = landing.at[pl.ds(0, devices - 1)]
        pltpu.make_async_copy(most, most, sem.at[phase]).wait()

    eye = lax.broadcasted_iota(jnp.int32, (LANES, LANES), 0) == lax.broadcasted_iota(
        jnp.int32, (LANES, LANES), 1
    )

    def to_col(row):
        return jnp.sum(jnp.where(eye, row, 0.0), axis=1, keepdims=True)

    def to_row(col):
        return jnp.sum(jnp.where(eye, col, 0.0), axis=0, keepdims=True)

    rounded = v_ref[...].astype(jnp.bfloat16)
    if pad_tiles > own_tiles:
        rounded = jnp.concatenate(
            [v_ref[...], jnp.zeros((pad_tiles - own_tiles, LANES), jnp.float32)], axis=0
        ).astype(jnp.bfloat16)
    v_send[...] = rounded
    v_all[me] = rounded
    pl.semaphore_wait(barrier, devices - 1)
    send_all(0, lambda other: v_send, v_all)

    loads[0].wait()
    loads[1].wait()
    for r in range(left.shape[0] // LANES):
        left_t[:, r * LANES : (r + 1) * LANES] = left[r * LANES : (r + 1) * LANES, :].T
    for t in range(own_tiles):
        right_t[:, t * LANES : (t + 1) * LANES] = right[t * LANES : (t + 1) * LANES, :].T
    rows = gram_send.shape[1]
    half = keep // rows
    gram = lax.dot_general(
        left_t[...], left_t[...], NT_DIMS, precision=HIGH, preferred_element_type=jnp.float32
    )
    gram_send[0:half] = gram.reshape(half, rows, keep)
    gram = lax.dot_general(
        right_t[...], right_t[...], NT_DIMS, precision=HIGH, preferred_element_type=jnp.float32
    )
    gram_send[half : 2 * half] = gram.reshape(half, rows, keep)
    gram_recv[me] = gram_send[lax.rem(me, chunks)]
    send_all(1, lambda other: gram_send.at[lax.rem(other, chunks)], gram_recv)

    cols_rows[...] = jnp.full(cols_rows.shape, -1.0, jnp.float32)
    for r in range(blocks):
        row = cols_ref[r : r + 1, :]
        alive = lax.broadcasted_iota(jnp.int32, (1, slots), 1) < count_ref[r]
        cols_rows[r : r + 1, 0:slots] = jnp.where(alive, row, -1).astype(jnp.float32)
    entries = picked.shape[0]
    lane = lax.broadcasted_iota(jnp.int32, (1, entries), 1)
    line = jnp.full((1, entries), -1.0, jnp.float32)
    for r in range(blocks):
        row = cols_rows[r : r + 1, :]
        if r:
            row = pltpu.roll(row, r * stride, 1)
        line = jnp.where((lane >= r * stride) & (lane < r * stride + slots), row, line)
    whole = line.astype(jnp.int32)
    pick_row = jnp.where(whole < 0, -1, whole // own_tiles * pad_tiles + whole % own_tiles)
    put_row = jnp.where(whole < 0, -1, whole // own_tiles * part_rows + whole % own_tiles)
    pick_col = to_col(pick_row.astype(jnp.float32)).astype(jnp.int32)
    pick_hot[...] = jnp.where(
        lax.broadcasted_iota(jnp.int32, pick_hot.shape, 1) == pick_col, 1.0, 0.0
    ).astype(jnp.bfloat16)
    put_hot[...] = jnp.where(
        lax.broadcasted_iota(jnp.int32, put_hot.shape, 0) == put_row, 1.0, 0.0
    ).astype(jnp.bfloat16)
    contrib[...] = jnp.zeros_like(contrib)

    wait_all(recv_sem, 0, v_all)
    picked[...] = jnp.dot(
        pick_hot[...],
        v_all[...].reshape(devices * pad_tiles, LANES),
        preferred_element_type=jnp.float32,
    )
    loads[2].wait()
    beta = beta_ref[0]

    def forward(r, carry):
        total = jnp.zeros((LANES, LANES), jnp.float32)
        for s in range(slots):
            total = total + tiles[r, s].astype(jnp.float32) * picked[pl.ds(r * stride + s, 1), :]
        q = to_row(jnp.sum(total, axis=1, keepdims=True))
        p_scr[pl.ds(r, 1), :] = q - beta * u_ref[pl.ds(r, 1), :]
        return carry

    lax.fori_loop(0, blocks, forward, 0)

    def start_dots(phase, basis_t, vec, count):
        total = jnp.zeros((keep, LANES), jnp.float32)
        for r in range(count):
            total = total + basis_t[:, r * LANES : (r + 1) * LANES] * vec[r : r + 1, :]
        dots = to_row(jnp.sum(total, axis=1, keepdims=True))
        square = jnp.sum(vec * vec, keepdims=True)
        both = jnp.concatenate([dots, jnp.broadcast_to(square, (1, LANES))], axis=0)
        side = phase // 4
        dot_send[side] = both
        dot_recv[side, me] = both
        send_all(phase, lambda other: dot_send.at[side], dot_recv.at[side])

    def finish_dots(phase, gram):
        side = phase // 4
        wait_all(recv_sem, phase, dot_recv.at[side])
        both = jnp.sum(dot_recv[side], axis=0)
        first, square = both[0:1, :], both[1:2, 0:1]
        coef = 2.0 * to_col(first) - jnp.sum(gram * first, axis=1, keepdims=True)
        coef_row = to_row(coef)
        spread = jnp.sum(gram * coef_row, axis=1, keepdims=True)
        total = (
            square
            - 2.0 * jnp.sum(coef_row * first, keepdims=True)
            + jnp.sum(coef * spread, keepdims=True)
        )
        return coef, jnp.sqrt(total + 1e-06)

    p = p_scr[0:blocks, :]
    start_dots(3, left_t, p, blocks)

    wait_all(recv_sem, 1, gram_recv)
    mine = jnp.sum(gram_recv[...], axis=0)
    gram_sum[...] = mine
    gram_all[me] = mine
    send_all(2, lambda other: gram_sum, gram_all)
    wait_all(recv_sem, 2, gram_all)

    coef, alpha = finish_dots(3, gram_all[0:half].reshape(keep, keep))
    out_coef[0] = alpha[0, 0]
    for r in range(blocks):
        fix = jnp.sum(left_t[:, r * LANES : (r + 1) * LANES] * coef, axis=0, keepdims=True)
        p_scr[r : r + 1, :] = (p[r : r + 1, :] - fix) / alpha
    out_left[...] = p_scr[0:blocks, :] * left_scale

    def backward(r, carry):
        row = p_scr[pl.ds(r, 1), :].astype(jnp.bfloat16).astype(jnp.float32)
        col = jnp.broadcast_to(to_col(row), (LANES, LANES))
        for g in range(0, slots, 8):
            lines = [
                jnp.sum(tiles[r, s].astype(jnp.float32) * col, axis=0, keepdims=True)
                for s in range(g, min(g + 8, slots))
            ]
            contrib[pl.ds(pl.multiple_of(r * stride + g, 8), len(lines)), :] = jnp.concatenate(
                lines, axis=0
            )
        return carry

    lax.fori_loop(0, blocks, backward, 0)
    rest = contrib[...]
    spread = jnp.zeros((devices * part_rows, LANES), jnp.float32)
    for _ in range(3):
        piece = rest.astype(jnp.bfloat16)
        rest = rest - piece.astype(jnp.float32)
        spread = spread + jnp.dot(put_hot[...], piece, preferred_element_type=jnp.float32)
    part_send[...] = spread.reshape(devices, part_rows, LANES)
    part_recv[me] = part_send[me]
    send_all(5, lambda other: part_send.at[other], part_recv)
    wait_all(recv_sem, 5, part_recv)
    own_scr[...] = jnp.sum(part_recv[...], axis=0)
    r_vec = own_scr[0:own_tiles, :] - alpha * v_ref[...]
    start_dots(4, right_t, r_vec, own_tiles)
    coef, beta_new = finish_dots(4, gram_all[half : 2 * half].reshape(keep, keep))
    out_coef[1] = beta_new[0, 0]
    for t in range(own_tiles):
        fix = jnp.sum(right_t[:, t * LANES : (t + 1) * LANES] * coef, axis=0, keepdims=True)
        out_right[t : t + 1, :] = (r_vec[t : t + 1, :] - fix) / beta_new * right_scale

    wait_all(send_sem, 0, v_all)
    wait_all(send_sem, 1, gram_recv)
    wait_all(send_sem, 2, gram_all)
    wait_all(send_sem, 3, dot_recv.at[0])
    wait_all(send_sem, 4, dot_recv.at[1])
    wait_all(send_sem, 5, part_recv)


def on_device(tiles, tile_cols, tile_count, u_start, v_start, beta_start, left_basis, right_basis):
    devices = lax.axis_size(AXES)
    planes = lax.axis_size("plane")
    blocks, slots = tile_cols.shape
    own_tiles = v_start.shape[0] // LANES
    left_rows, keep = left_basis.shape
    right_rows = right_basis.shape[0]
    pad_tiles = -(-own_tiles // 16) * 16
    part_rows = -(-own_tiles // 8) * 8
    rows = max(8, 2 * keep // devices)
    chunks = 2 * keep // rows
    stride = -(-slots // 8) * 8
    while (blocks * stride) % LANES:
        stride += 8
    entries = blocks * stride
    f32, bf16 = jnp.float32, jnp.bfloat16
    vmem = pl.BlockSpec(memory_space=pltpu.VMEM)
    smem = pl.BlockSpec(memory_space=pltpu.SMEM)
    hbm = pl.BlockSpec(memory_space=pl.ANY)
    left_out, right_out, coefs = pl.pallas_call(
        functools.partial(
            steps_kernel,
            devices,
            planes,
            own_tiles,
            math.sqrt(left_rows * devices),
            math.sqrt(right_rows * devices),
        ),
        out_shape=(
            jax.ShapeDtypeStruct((blocks, LANES), f32),
            jax.ShapeDtypeStruct((own_tiles, LANES), f32),
            jax.ShapeDtypeStruct((2,), f32),
        ),
        in_specs=[smem, smem, vmem, vmem, vmem, hbm, hbm, hbm],
        out_specs=(vmem, vmem, smem),
        scratch_shapes=[
            pltpu.VMEM(tiles.shape, bf16),
            pltpu.VMEM(left_basis.shape, f32),
            pltpu.VMEM(right_basis.shape, f32),
            pltpu.VMEM((keep, left_rows), f32),
            pltpu.VMEM((keep, right_rows), f32),
            pltpu.VMEM((pad_tiles, LANES), bf16),
            pltpu.VMEM((devices, pad_tiles, LANES), bf16),
            pltpu.VMEM((-(-blocks // 8) * 8, entries), f32),
            pltpu.VMEM((entries, devices * pad_tiles), bf16),
            pltpu.VMEM((devices * part_rows, entries), bf16),
            pltpu.VMEM((entries, LANES), f32),
            pltpu.VMEM((entries, LANES), f32),
            pltpu.VMEM((chunks, rows, keep), f32),
            pltpu.VMEM((devices, rows, keep), f32),
            pltpu.VMEM((rows, keep), f32),
            pltpu.VMEM((devices, rows, keep), f32),
            pltpu.VMEM((2, 2, keep), f32),
            pltpu.VMEM((2, devices, 2, keep), f32),
            pltpu.VMEM((devices, part_rows, LANES), f32),
            pltpu.VMEM((devices, part_rows, LANES), f32),
            pltpu.VMEM((part_rows, LANES), f32),
            pltpu.VMEM((-(-blocks // 8) * 8, LANES), f32),
            pltpu.SemaphoreType.DMA((3,)),
            pltpu.SemaphoreType.DMA((6,)),
            pltpu.SemaphoreType.DMA((6,)),
        ],
        compiler_params=pltpu.CompilerParams(
            collective_id=0, has_side_effects=True, vmem_limit_bytes=60 * 1024 * 1024
        ),
    )(
        beta_start,
        tile_count,
        tile_cols,
        u_start.reshape(blocks, LANES),
        v_start.reshape(own_tiles, LANES),
        tiles,
        left_basis,
        right_basis,
    )
    return left_out.reshape(1, -1), right_out.reshape(1, -1), coefs


def solution(mesh):
    placed = (
        P(AXES, None, None, None),
        P(AXES, None),
        P(AXES),
        P(AXES),
        P(AXES),
        P(),
        P(AXES, None),
        P(AXES, None),
    )
    return jax.shard_map(
        on_device,
        mesh=mesh,
        in_specs=placed,
        out_specs=(P(None, AXES), P(None, AXES), P()),
        check_vma=False,
    )
```

time: 340 us -> 42.9 us (0.13)
  waiting for transfers between devices: 171 us -> 0 us
  blocking collectives: 118 us -> 0 us
  Pallas kernels: 0 us -> 37.6 us
  matrix products: 19.5 us -> 0 us
  between operations: 18.8 us -> 1.29 us
  other arithmetic: 8.19 us -> 0 us
    reduce_scatter x1 -> x0, waiting for transfers between devices: 134 us -> none  [on_device(): lax.psum_scatter(partial_value, ('blk', 'plane'), scatter_dimension=0, ti...]
    psum x2 -> x0, blocking collectives: 74.3 us -> none  [project_twice(): lax.psum((jnp.dot(vec, basis, precision=high), jnp.sum(vec * vec)), ('blk...]
    all_gather x1 -> x0, blocking collectives: 43.6 us -> none  [on_device(): whole = lax.all_gather(rounded, ('blk', 'plane'), axis=0, tiled=True)]
    pallas_call x0 -> x1, Pallas kernels: none -> 37.6 us  [on_device(): pl.pallas_call(functools.partial(steps_kernel, devices, planes, own_tiles...]
    psum x1 -> x0, waiting for transfers between devices: 37.2 us -> none  [on_device(): lax.psum((jnp.dot(left_basis.T, left_basis, precision=high), jnp.dot(righ...]
    dot_general x13 -> x0, matrix products: 19.5 us -> none  [the longest x1 4.1 us: on_device(): jnp.dot(right_basis.T, right_basis, precision=high)]
    unnamed x8 -> x3, local copies, waits for them, and re-layouts: 0.02 us -> 3.7 us
  transfers between devices with their start and end apart: 2 -> 0, of which waited for: 2 -> 0; matrix products, arithmetic and copies ran while one was open for 3% -> 0% of each run, Pallas kernels for 0% -> 0%
where the time goes in v1:
time: 42.9 us; the launch traced here: 42.6 us
  Pallas kernels  37.6 us (88%)
  local copies, waits for them, and re-layouts  3.7 us (9%)
  between operations  1.29 us (3%)
    pallas_call x1, Pallas kernels, on_device(): pl.pallas_call(functools.partial(steps_kernel, devices, planes, own_tiles...  37.6 us
    unnamed x3, local copies, waits for them, and re-layouts  3.7 us

profile of v1, /device:TPU:0, one launch (start us, length us, event | category | flops | bytes accessed | tf_op | source)
XLA Modules:
  0.0 42.6 jit_solution(14939496421415141736)
XLA Ops:
  1.3 37.6 %shard_map.103 = (f32[4,128]{1,0:T(4,128)}, f32[16,128]{1,0:T(8,128)}, f32[2]{0:T(128)}) custom-call(f32[1]{0:T(128)S(6)} %copy.14.beta_ref, s32[4]{0:T(128)} %count_ref.1, s32[4,24]{1,0:T(4,128)} %cols_ref.1, f32[4,128]{1,0:T(4,128)} %bitcast.6, f32[16,128]{1,0:T(8,128)} %bitcast.4, bf16[4,24,128,128]{3,2,1,0:T(8,128)(2,1)} %tiles_hbm.1, ...), custom_call_target="tpu_custom_call" | custom-call | tf_op jit(solution)/shard_map/pallas_call | solution.py:298
  38.9 1.2 %copy.15 = f32[1,512]{1,0:T(1,128)} copy(f32[1,512]{1,0:T(1,128)} %bitcast.7) | data formatting | bytes 4096
  40.1 1.3 %copy.16 = f32[1,2048]{1,0:T(1,128)} copy(f32[1,2048]{1,0:T(1,128)} %bitcast.5) | data formatting | bytes 16384
  41.4 1.2 %copy.17 = f32[2]{0:T(128)} copy(f32[2]{0:T(128)} %get-tuple-element.14) | data formatting | bytes 16
